TPU v7x, 32 devices: a whole 2x2x4 slice. The times are simulated.
32 devices in a mesh: expert: 4 (over z), tensor: 8 (over y, x, core).
Axes of the slice: x: 2, y: 2, z: 4, core: 2. Of those that a mesh axis runs over, the one named last changes fastest.
Arguments:
- layer_input: bfloat16 [8192, 2048], P('expert'), may hold values from -6 to 6
- cotangent: bfloat16 [8192, 2048], P(('expert', 'tensor')), may hold values from -6 to 6
- lengths: int32 [4, 4], P('expert'), may hold values from 1 to 1024, 2048 in all within a row
- routes: int32 [8192, 8], P(('expert', 'tensor')), may hold values from 0 to 15, all different within a row; in each aligned block of 256 rows (0 to 255, 256 to 511, ...) at most 192 rows name the same one
- attn_gain: float32 [2048], replicated, may hold values from 0.5 to 1.5
- w_qkv: bfloat16 [2048, 3, 2048], P(None, None, 'tensor'), may hold values from -0.125 to 0.125
- q_gain: float32 [128], replicated, may hold values from 0.6 to 5
- k_gain: float32 [128], replicated, may hold values from 0.6 to 5
- w_out: bfloat16 [2048, 2048], P('tensor'), may hold values from -2 to 2
- ffn_gain: float32 [2048], replicated, may hold values from 0.5 to 1.5
- w_router: bfloat16 [2048, 16], replicated, may hold values from -0.125 to 0.125
- w_gate: bfloat16 [16, 2048, 1024], P('expert', None, 'tensor'), may hold values from -0.125 to 0.125
- w_up: bfloat16 [16, 2048, 1024], P('expert', None, 'tensor'), may hold values from -0.125 to 0.125
- w_down: bfloat16 [16, 1024, 2048], P('expert', 'tensor'), may hold values from -6 to 6
Outputs:
- output: bfloat16 [8192, 2048], P(('expert', 'tensor'))
- grad_input: bfloat16 [8192, 2048], P(('expert', 'tensor'))
- grad_attn_gain: float32 [2048], replicated
- grad_w_qkv: float32 [2048, 3, 2048], P(None, None, 'tensor')
- grad_q_gain: float32 [128], replicated
- grad_k_gain: float32 [128], replicated
- grad_w_out: float32 [2048, 2048], P('tensor')
- grad_ffn_gain: float32 [2048], replicated
- grad_w_router: float32 [2048, 16], replicated
- grad_w_gate: float32 [16, 2048, 1024], P('expert', None, 'tensor')
- grad_w_up: float32 [16, 2048, 1024], P('expert', None, 'tensor')
- grad_w_down: float32 [16, 1024, 2048], P('expert', 'tensor')
Inputs may be any that keep to these rules, and one draw needn't show every extreme that they name: `routes`: no expert is named by more than 192 of the 256 rows of one device (aligned blocks of rows); in every draw some expert is named 192 times in some block. `lengths`: each row sums to 2048; its longest sequence has exactly 1024 tokens.
All inputs are finite; a program needn't handle non-finite values.
Results may differ from a plain program's by a relative error of at most 0.024.
The roundings to bfloat16 on the way count: a program that leaves them out, or rounds other values in their place, can miss the bound.
Values may be sent and summed in bfloat16 or wider, within the bound.
A program may use at most 384 MiB of HBM per device.

v0:
```python
import math
import jax
import jax.numpy as jnp
from jax import lax
from jax.sharding import PartitionSpec as P

NORM_EPS = 1e-06
ROPE_BASE = 50000.0


def rms_scale(values):
    return lax.rsqrt(jnp.mean(values * values, axis=-1, keepdims=True) + NORM_EPS)


def positions_of(seq_lengths, row_count):
    seq_ends = jnp.cumsum(seq_lengths)
    starts = seq_ends - seq_lengths
    row_index = jnp.arange(row_count, dtype=jnp.int32)
    segment = jnp.sum((row_index[:, None] >= seq_ends[None, :]).astype(jnp.int32), axis=1)
    picked = segment[:, None] == jnp.arange(seq_lengths.shape[0], dtype=jnp.int32)[None, :]
    offsets = jnp.sum(jnp.where(picked, starts[None, :], 0), axis=1)
    return (segment, row_index - offsets)


def rotate(values, position):
    half_width = values.shape[-1] // 2
    frequency = jnp.exp(
        jnp.arange(half_width, dtype=jnp.float32) * (-2.0 * math.log(ROPE_BASE) / values.shape[-1])
    )
    angle = position.astype(jnp.float32)[:, None] * frequency[None, :]
    cosine = jnp.cos(angle)[:, None, :]
    sine_part = jnp.sin(angle)[:, None, :]
    first_half = values[..., :half_width]
    second = values[..., half_width:]
    return jnp.concatenate(
        [first_half * cosine - second * sine_part, second * cosine + first_half * sine_part],
        axis=-1,
    )


def shape_heads(qkv_proj, q_gain, k_gain, position):
    query_rows = qkv_proj[:, 0]
    key_rows = qkv_proj[:, 1]
    value_rows = qkv_proj[:, 2]
    query_rows = rotate(query_rows * rms_scale(query_rows) * q_gain, position)
    key_rows = rotate(key_rows * rms_scale(key_rows) * k_gain, position)
    return (query_rows, key_rows, value_rows)


def masked_scores(query_block, key_rows, segment_block, segment, score_scale):
    scores = (
        jnp.einsum("qhd,khd->hqk", query_block, key_rows, preferred_element_type=jnp.float32)
        * score_scale
    )
    same_seq = (segment_block[:, None] == segment[None, :])[None]
    return jnp.where(same_seq, scores, -1e30)


def attend_forward(query_rows, key_rows, value_rows, segment, block_rows, score_scale):
    row_count, head_count, head_width = query_rows.shape
    block_count = row_count // block_rows

    def one_block(block_item):
        query_block, segment_block = block_item
        scores = masked_scores(query_block, key_rows, segment_block, segment, score_scale)
        row_peak = jnp.max(scores, axis=-1, keepdims=True)
        weights = jnp.exp(scores - row_peak)
        row_total = jnp.sum(weights, axis=-1, keepdims=True)
        probabilities = (weights / row_total).astype(jnp.bfloat16)
        mixed_out = jnp.einsum(
            "hqk,khd->qhd", probabilities, value_rows, preferred_element_type=jnp.float32
        )
        return (mixed_out, (row_peak + jnp.log(row_total))[..., 0])

    blocks = (
        query_rows.reshape(block_count, block_rows, head_count, head_width),
        segment.reshape(block_count, block_rows),
    )
    mixed_out, log_total = lax.map(one_block, blocks)
    return (mixed_out.reshape(row_count, head_count, head_width), log_total)


def attend_backward(
    query_rows, key_rows, value_rows, segment, grad_mixed, log_total, block_rows, score_scale
):
    row_count, head_count, head_width = query_rows.shape
    block_count = row_count // block_rows

    def one_block(carry, block_item):
        grad_keys, grad_values = carry
        query_block, segment_block, grad_block, total_block = block_item
        scores = masked_scores(query_block, key_rows, segment_block, segment, score_scale)
        probabilities = jnp.exp(scores - total_block[..., None])
        grad_probs = jnp.einsum(
            "qhd,khd->hqk", grad_block, value_rows, preferred_element_type=jnp.float32
        )
        delta = jnp.sum(grad_probs * probabilities, axis=-1, keepdims=True)
        grad_scores = (probabilities * (grad_probs - delta)).astype(jnp.bfloat16)
        grad_query = (
            jnp.einsum("hqk,khd->qhd", grad_scores, key_rows, preferred_element_type=jnp.float32)
            * score_scale
        )
        grad_keys = (
            grad_keys
            + jnp.einsum(
                "hqk,qhd->khd", grad_scores, query_block, preferred_element_type=jnp.float32
            )
            * score_scale
        )
        grad_values = grad_values + jnp.einsum(
            "hqk,qhd->khd",
            probabilities.astype(jnp.bfloat16),
            grad_block,
            preferred_element_type=jnp.float32,
        )
        return ((grad_keys, grad_values), grad_query)

    blocks = (
        query_rows.reshape(block_count, block_rows, head_count, head_width),
        segment.reshape(block_count, block_rows),
        grad_mixed.reshape(block_count, block_rows, head_count, head_width),
        log_total,
    )
    start_carry = (jnp.zeros(key_rows.shape, jnp.float32), jnp.zeros(value_rows.shape, jnp.float32))
    (grad_keys, grad_values), grad_query = lax.scan(one_block, start_carry, blocks)
    return (grad_query.reshape(row_count, head_count, head_width), grad_keys, grad_values)


def swiglu_back(grad_hidden, gate_pre, up_pre):
    sigmoid = jax.nn.sigmoid(gate_pre)
    grad_gate = grad_hidden * up_pre * sigmoid * (1.0 + gate_pre * (1.0 - sigmoid))
    grad_up = grad_hidden * gate_pre * sigmoid
    return (grad_gate.astype(jnp.bfloat16), grad_up.astype(jnp.bfloat16))


def body(
    layer_input,
    cotangent,
    lengths,
    routes,
    attn_gain,
    w_qkv,
    q_gain,
    k_gain,
    w_out,
    ffn_gain,
    w_router,
    w_gate,
    w_up,
    w_down,
):
    group_rows, model_width = layer_input.shape
    own_rows, top_count = routes.shape
    head_width = q_gain.shape[0]
    local_heads = w_qkv.shape[2] // head_width
    experts_all = w_router.shape[1]
    experts_here = w_gate.shape[0]
    senders = lax.axis_size("expert")
    tensor_rank = lax.axis_index("tensor")
    capacity = max(2, 3 * own_rows * top_count // (2 * experts_all))
    block_rows = min(512, group_rows)
    score_scale = 1.0 / math.sqrt(head_width)
    input_full = layer_input.astype(jnp.float32)
    scale_one = rms_scale(input_full)
    normed = (input_full * scale_one * attn_gain).astype(jnp.bfloat16)
    qkv_weight = w_qkv.reshape(model_width, 3 * local_heads * head_width)
    qkv_proj = jnp.dot(normed, qkv_weight, preferred_element_type=jnp.float32).reshape(
        group_rows, 3, local_heads, head_width
    )
    segment, position = positions_of(lengths[0], group_rows)

    def head_shapes(raw_proj, gain_q, gain_k):
        return shape_heads(raw_proj, gain_q, gain_k, position)

    (query_full, key_full, value_full), head_back = jax.vjp(head_shapes, qkv_proj, q_gain, k_gain)
    query_low = query_full.astype(jnp.bfloat16)
    key_low = key_full.astype(jnp.bfloat16)
    value_low = value_full.astype(jnp.bfloat16)
    mixed_full, log_total = attend_forward(
        query_low, key_low, value_low, segment, block_rows, score_scale
    )
    mixed_low = mixed_full.astype(jnp.bfloat16).reshape(group_rows, local_heads * head_width)
    row_part = mixed_low
    attn_own = lax.psum_scatter(
        jnp.dot(row_part, w_out, preferred_element_type=jnp.float32),
        "tensor",
        scatter_dimension=0,
        tiled=True,
    )
    input_own = lax.dynamic_slice_in_dim(input_full, tensor_rank * own_rows, own_rows, 0)
    scale_own = lax.dynamic_slice_in_dim(scale_one, tensor_rank * own_rows, own_rows, 0)
    residual = input_own + attn_own
    scale_two = rms_scale(residual)
    ffn_in = (residual * scale_two * ffn_gain).astype(jnp.bfloat16)
    logits = jnp.dot(ffn_in, w_router, preferred_element_type=jnp.float32)
    probabilities = jax.nn.softmax(logits, axis=-1)
    chosen = routes[:, :, None] == jnp.arange(experts_all, dtype=jnp.int32)[None, None, :]
    gate_weights = jnp.sum(jnp.where(chosen, probabilities[:, None, :], 0.0), axis=-1)
    grad_output = cotangent.astype(jnp.float32)
    flat_routes = routes.reshape(-1)
    expert_hits = (
        flat_routes[:, None] == jnp.arange(experts_all, dtype=jnp.int32)[None, :]
    ).astype(jnp.int32)
    slot_index = jnp.sum(expert_hits * (jnp.cumsum(expert_hits, axis=0) - 1), axis=1)
    spread_in = jnp.broadcast_to(ffn_in[:, None, :], (own_rows, top_count, model_width)).reshape(
        -1, model_width
    )
    spread_grad = (
        (gate_weights[:, :, None] * grad_output[:, None, :])
        .astype(jnp.bfloat16)
        .reshape(-1, model_width)
    )
    send_in = (
        jnp.zeros((experts_all, capacity, model_width), jnp.bfloat16)
        .at[flat_routes, slot_index]
        .set(spread_in)
    )
    send_grad = (
        jnp.zeros((experts_all, capacity, model_width), jnp.bfloat16)
        .at[flat_routes, slot_index]
        .set(spread_grad)
    )
    layout = (senders, experts_here, capacity, model_width)
    recv_rows, expert_grad = (
        lax.all_to_all(send_in.reshape(layout), "expert", split_axis=0, concat_axis=0, tiled=True),
        lax.all_to_all(
            send_grad.reshape(layout), "expert", split_axis=0, concat_axis=0, tiled=True
        ),
    )
    gate_full, up_full, down_full = (
        lax.all_gather(w_gate, "tensor", axis=2, tiled=True),
        lax.all_gather(w_up, "tensor", axis=2, tiled=True),
        lax.all_gather(w_down, "tensor", axis=1, tiled=True),
    )
    gate_all = jnp.einsum(
        "sctd,cdf->sctf", recv_rows, gate_full, preferred_element_type=jnp.float32
    )
    up_all = jnp.einsum("sctd,cdf->sctf", recv_rows, up_full, preferred_element_type=jnp.float32)
    hidden_low = (jax.nn.silu(gate_all) * up_all).astype(jnp.bfloat16)
    expert_out = jnp.einsum(
        "sctf,cfd->sctd", hidden_low, down_full, preferred_element_type=jnp.float32
    ).astype(jnp.bfloat16)
    grad_hidden = jnp.einsum(
        "sctd,cfd->sctf", expert_grad, down_full, preferred_element_type=jnp.float32
    )
    grad_gate_pre, grad_up_pre = swiglu_back(grad_hidden, gate_all, up_all)
    whole_down = jnp.einsum(
        "sctf,sctd->cfd", hidden_low, expert_grad, preferred_element_type=jnp.float32
    )
    whole_gate = jnp.einsum(
        "sctd,sctf->cdf", recv_rows, grad_gate_pre, preferred_element_type=jnp.float32
    )
    whole_up = jnp.einsum(
        "sctd,sctf->cdf", recv_rows, grad_up_pre, preferred_element_type=jnp.float32
    )
    from_gate = jnp.einsum(
        "sctf,cdf->sctd", grad_gate_pre, gate_full, preferred_element_type=jnp.float32
    )
    from_up = jnp.einsum("sctf,cdf->sctd", grad_up_pre, up_full, preferred_element_type=jnp.float32)
    grad_inputs = (from_gate + from_up).astype(jnp.bfloat16)
    grad_gate, grad_up, grad_down = (
        lax.psum_scatter(
            whole_gate.astype(jnp.bfloat16), "tensor", scatter_dimension=2, tiled=True
        ).astype(jnp.float32),
        lax.psum_scatter(
            whole_up.astype(jnp.bfloat16), "tensor", scatter_dimension=2, tiled=True
        ).astype(jnp.float32),
        lax.psum_scatter(
            whole_down.astype(jnp.bfloat16), "tensor", scatter_dimension=1, tiled=True
        ).astype(jnp.float32),
    )
    back_rows, back_grads = (
        lax.all_to_all(expert_out, "expert", split_axis=0, concat_axis=0, tiled=True),
        lax.all_to_all(grad_inputs, "expert", split_axis=0, concat_axis=0, tiled=True),
    )
    pick_index = flat_routes * capacity + slot_index
    rows_back = (
        back_rows.reshape(experts_all * capacity, model_width)[pick_index]
        .reshape(own_rows, top_count, model_width)
        .astype(jnp.float32)
    )
    grads_back = (
        back_grads.reshape(experts_all * capacity, model_width)[pick_index]
        .reshape(own_rows, top_count, model_width)
        .astype(jnp.float32)
    )
    mixture = jnp.sum(gate_weights[:, :, None] * rows_back, axis=1)
    output = (residual + mixture).astype(jnp.bfloat16)
    grad_gates = jnp.sum(grad_output[:, None, :] * rows_back, axis=-1)
    grad_probs = jnp.sum(jnp.where(chosen, grad_gates[:, :, None], 0.0), axis=1)
    grad_logits = (
        probabilities * (grad_probs - jnp.sum(grad_probs * probabilities, axis=-1, keepdims=True))
    ).astype(jnp.bfloat16)
    router_part = lax.dot_general(
        ffn_in, grad_logits, (((0,), (0,)), ((), ())), preferred_element_type=jnp.float32
    )
    grad_ffn = jnp.sum(grads_back, axis=1) + lax.dot_general(
        grad_logits, w_router, (((1,), (1,)), ((), ())), preferred_element_type=jnp.float32
    )
    ffn_gain_part = jnp.sum(grad_ffn * residual * scale_two, axis=0)
    scaled_two = grad_ffn * ffn_gain
    grad_residual = grad_output + scale_two * (
        scaled_two
        - residual * scale_two * scale_two * jnp.mean(scaled_two * residual, axis=-1, keepdims=True)
    )
    grad_attn = grad_residual.astype(jnp.bfloat16)
    shard_part = lax.all_gather(grad_attn, "tensor", axis=0, tiled=True)
    grad_weight = lax.dot_general(
        mixed_low, shard_part, (((0,), (0,)), ((), ())), preferred_element_type=jnp.float32
    )
    grad_rows_part = lax.dot_general(
        shard_part, w_out, (((1,), (1,)), ((), ())), preferred_element_type=jnp.float32
    ).astype(jnp.bfloat16)
    grad_mixed = grad_rows_part
    out_part, grad_mixed = (grad_weight, grad_mixed)
    grad_query, grad_keys, grad_values = attend_backward(
        query_low,
        key_low,
        value_low,
        segment,
        grad_mixed.reshape(group_rows, local_heads, head_width),
        log_total,
        block_rows,
        score_scale,
    )
    grad_qkv, q_gain_part, k_gain_part = head_back((grad_query, grad_keys, grad_values))
    grad_qkv_low = grad_qkv.astype(jnp.bfloat16).reshape(group_rows, 3 * local_heads * head_width)
    qkv_part = lax.dot_general(
        normed, grad_qkv_low, (((0,), (0,)), ((), ())), preferred_element_type=jnp.float32
    ).reshape(w_qkv.shape)
    row_part = grad_qkv_low
    grad_normed = lax.psum_scatter(
        lax.dot_general(
            row_part, qkv_weight, (((1,), (1,)), ((), ())), preferred_element_type=jnp.float32
        ).astype(jnp.bfloat16),
        "tensor",
        scatter_dimension=0,
        tiled=True,
    ).astype(jnp.float32)
    attn_gain_part = jnp.sum(grad_normed * input_own * scale_own, axis=0)
    scaled_one = grad_normed * attn_gain
    grad_input = grad_residual + scale_own * (
        scaled_one
        - input_own
        * scale_own
        * scale_own
        * jnp.mean(scaled_one * input_own, axis=-1, keepdims=True)
    )
    grad_qkv_sum, grad_out_sum = (
        lax.psum(qkv_part.astype(jnp.bfloat16), "expert").astype(jnp.float32),
        lax.psum(out_part.astype(jnp.bfloat16), "expert").astype(jnp.float32),
    )
    grad_attn_gain, grad_q_gain, grad_k_gain, grad_ffn_gain, grad_router = lax.psum(
        (attn_gain_part, q_gain_part, k_gain_part, ffn_gain_part, router_part), ("expert", "tensor")
    )
    return (
        output,
        grad_input.astype(jnp.bfloat16),
        grad_attn_gain,
        grad_qkv_sum,
        grad_q_gain,
        grad_k_gain,
        grad_out_sum,
        grad_ffn_gain,
        grad_router,
        grad_gate,
        grad_up,
        grad_down,
    )


def solution(mesh):
    in_specs = (
        P("expert", None),
        P(("expert", "tensor"), None),
        P("expert", None),
        P(("expert", "tensor"), None),
        P(),
        P(None, None, "tensor"),
        P(),
        P(),
        P("tensor", None),
        P(),
        P(),
        P("expert", None, "tensor"),
        P("expert", None, "tensor"),
        P("expert", "tensor", None),
    )
    out_specs = (
        P(("expert", "tensor"), None),
        P(("expert", "tensor"), None),
        P(),
        P(None, None, "tensor"),
        P(),
        P(),
        P("tensor", None),
        P(),
        P(),
        P("expert", None, "tensor"),
        P("expert", None, "tensor"),
        P("expert", "tensor", None),
    )
    return jax.shard_map(body, mesh=mesh, in_specs=in_specs, out_specs=out_specs, check_vma=False)
```

profile of v0, /device:TPU:0, one launch (start us, length us, event | category | flops | bytes accessed | tf_op | source)
XLA Modules:
  0.0 2259.6 jit_solution(2812571986861035458)
XLA Ops:
  49.6 41.2 %while.27 = (s32[]{:T(128)}, bf16[4,512,2,128]{3,1,2,0:T(8,128)(2,1)}, f32[4,2,512]{2,1,0:T(2,128)}, s32[4,512]{1,0:T(4,128)S(1)}, s32[2048]{0:T(1024)S(1)}, /*i...) while((s32[]{:T(128)}, ...), condition=%wide.region_9.10_spmd, body=%wide.region_6.9_spmd.sunk | while | flops 1099955200 | bytes 32292448 | solution.py:79
  104.7 14.1 convert_element_type.146
  125.6 96.5 %reduce-scatter.10.cloned.1.call-done = f32[256,2048]{1,0:T(8,128)} async-done(((f32[2048,2048]{1,0:T(8,128)}), f32[256,2048]{1,0:T(8,128)}) %reduce-scatter.10.cloned.1.call-update) | async-done | bytes 2097168 | tf_op jit(solution)/shard_map/reduce_scatter | solution.py:184
  226.3 19.1 scatter_custom_fusion
  257.2 19.8 scatter_custom_fusion.1
  277.0 247.9 %all-to-all-done = bf16[4,4,192,2048]{3,2,1,0:T(8,128)(2,1)} async-done(((bf16[4,4,192,2048]{3,2,1,0:T(8,128)(2,1)}), bf16[4,4,192,2048]{3,2,1,0:T(8,128)(2,1)}, u32[]{:S(2)}, u32[]{:S(2)}) %all-to-all-start) | async-done | bytes 12582944 | tf_op jit(solution)/shard_map/all_to_all | solution.py:225
  531.7 22.6 %fusion.42 = f32[4,4,192,1024]{3,2,1,0:T(8,128)} fusion(bf16[4,2048,1024]{2,1,0:T(8,128)(2,1)} %all-gather.5.cloned.1.call-done, bf16[4,4,192,2048]{3,2,1,0:T(8,128)(2,1)} %all-to-all-done), kind=kOutput, calls=%fused_computation.64 | convolution fusion | flops 12884901888 | bytes 41943040 | tf_op jit(solution)/shard_map/sctd,cdf->sctf/dot_general | solution.py:235
  554.4 22.6 %fusion.38 = f32[4,4,192,1024]{3,2,1,0:T(8,128)} fusion(bf16[4,2048,1024]{2,1,0:T(8,128)(2,1)} %all-gather.7.cloned.1.call-done, bf16[4,4,192,2048]{3,2,1,0:T(8,128)(2,1)} %all-to-all-done), kind=kOutput, calls=%fused_computation.60 | convolution fusion | flops 12884901888 | bytes 41943040 | tf_op jit(solution)/shard_map/sctd,cdf->sctf/dot_general | solution.py:238
  577.0 227.2 %all-to-all-done.2 = bf16[4,4,192,2048]{3,2,1,0:T(8,128)(2,1)} async-done(((bf16[4,4,192,2048]{3,2,1,0:T(8,128)(2,1)}), bf16[4,4,192,2048]{3,2,1,0:T(8,128)(2,1)}, u32[]{:S(2)}, u32[]{:S(2)}) %all-to-all-start.2) | async-done | bytes 12582944 | tf_op jit(solution)/shard_map/all_to_all | solution.py:226
  804.2 31.3 %fusion.52 = (bf16[4,4,192,1024]{3,2,0,1:T(8,128)(2,1)}, bf16[4,4,192,1024]{3,2,0,1:T(8,128)(2,1)}, bf16[4,4,192,1024]{3,2,0,1:T(8,128)(2,1)}) fusion(f32[4,4,192,1024]{3,2,1,0:T(8,128)} %fusion.38, f32[4,4,192,1024]{3,2,1,0:T(8,128)} %fusion.42, bf16[4,1024,2048]{2,1,0:T(8,128)(2,1)} %all-gather.9.cloned.1.call-done, ...), kind=kOutput, calls=%fused_computation.79 | convolution fusion | flops 12935233536 | bytes 73400320 | tf_op jit(solution)/shard_map/sctd,cfd->sctf/dot_general | solution.py:243
  835.5 22.9 %convert_bitcast_fusion = bf16[4,4,192,2048]{3,2,0,1:T(8,128)(2,1)} fusion(bf16[4,4,192,1024]{3,2,0,1:T(8,128)(2,1)} %get-tuple-element.315, bf16[4,1024,2048]{2,1,0:T(8,128)(2,1)} %all-gather.9.cloned.1.call-done), kind=kOutput, calls=%fused_computation.91 | convolution fusion | flops 12891193344 | bytes 35651584 | tf_op jit(solution)/shard_map/sctf,cfd->sctd/dot_general | solution.py:240
  875.5 21.8 fusion.36
  897.3 24.3 %fusion.49 = bf16[4,4,192,2048]{3,2,0,1:T(8,128)(2,1)} fusion(f32[4,4,192,2048]{3,2,1,0:T(8,128)} %fusion.36, bf16[4,4,192,1024]{3,2,0,1:T(8,128)(2,1)} %get-tuple-element.314, bf16[4,2048,1024]{2,1,0:T(8,128)(2,1)} %all-gather.5.cloned.1.call-done), kind=kOutput, calls=%fused_computation.74 | convolution fusion | flops 12897484800 | bytes 60817408 | tf_op jit(solution)/shard_map/sctf,cdf->sctd/dot_general | solution.py:256
  932.3 215.7 %all-to-all-done.1 = bf16[4,4,192,2048]{3,2,1,0:T(8,128)(2,1)} async-done(((bf16[4,4,192,2048]{3,2,1,0:T(8,128)(2,1)}), bf16[4,4,192,2048]{3,2,1,0:T(8,128)(2,1)}, u32[]{:S(2)}, u32[]{:S(2)}) %all-to-all-start.1) | async-done | bytes 12582944 | tf_op jit(solution)/shard_map/all_to_all | solution.py:273
  1154.4 22.9 %gather_fusion = bf16[2048,2048]{1,0:T(8,128)(2,1)} fusion(bf16[3072,2048]{1,0:T(8,128)(2,1)} %bitcast.30, s32[2048]{0:T(1024)S(1)} %broadcast_clamp_fusion), kind=kCustom, calls=%fused_computation | custom fusion | bytes 16785408 | tf_op jit(solution)/shard_map/gather | solution.py:278
  1187.0 239.8 %all-to-all-done.3 = bf16[4,4,192,2048]{3,2,1,0:T(8,128)(2,1)} async-done(((bf16[4,4,192,2048]{3,2,1,0:T(8,128)(2,1)}), bf16[4,4,192,2048]{3,2,1,0:T(8,128)(2,1)}, u32[]{:S(2)}, u32[]{:S(2)}) %all-to-all-start.3) | async-done | bytes 12582944 | tf_op jit(solution)/shard_map/all_to_all | solution.py:274
  1426.8 22.9 %gather_fusion.1 = bf16[2048,2048]{1,0:T(8,128)(2,1)} fusion(bf16[3072,2048]{1,0:T(8,128)(2,1)} %bitcast.40, s32[2048]{0:T(1024)S(1)} %broadcast_clamp_fusion), kind=kCustom, calls=%fused_computation.1 | custom fusion | bytes 16785408 | tf_op jit(solution)/shard_map/gather | solution.py:283
  1449.8 11.4 convert_reduce_fusion
  1467.4 19.8 bitcast_convert_fusion.2
  1487.2 28.9 %copy.149 = bf16[4,2048,1024]{1,0,2:T(4,128)(2,1)} copy(bf16[4,2048,1024]{2,1,0:T(8,128)(2,1)} %bitcast_convert_fusion.2) | data formatting | bytes 33554432
  1516.0 18.6 copy.184
  1534.7 20.5 bitcast_convert_fusion.1
  1555.2 29.2 %copy.151 = bf16[4,2048,1024]{1,0,2:T(4,128)(2,1)} copy(bf16[4,2048,1024]{2,1,0:T(8,128)(2,1)} %bitcast_convert_fusion.1) | data formatting | bytes 33554432
  1584.4 18.9 copy.185
  1603.4 21.6 bitcast_convert_fusion
  1632.1 165.0 %while.28 = (s32[]{:T(128)}, f32[2048,2,128]{0,2,1:T(8,128)}, f32[2048,2,128]{0,2,1:T(8,128)}, f32[4,512,2,128]{1,0,3,2:T(4,128)}, bf16[4,512,2,128]{3,1,2,0:T(8...) while((s32[]{:T(128)}, f32[2048,2,128]{0,2,1:T(8,128)}, ...), condition=%wide.region_28.29_spmd.clone, body=%wide.region_26.28_spmd.clone.sunk | while | flops 2719611904 | bytes 170962192 | solution.py:125
  1824.8 11.8 convolution_convert_fusion
  1859.3 29.5 %reduce-scatter.14.cloned.1.call-done = bf16[4,128,2048]{2,1,0:T(8,128)(2,1)} async-done(((bf16[4,1024,2048]{2,1,0:T(8,128)(2,1)}), bf16[4,128,2048]{2,1,0:T(8,128)(2,1)}) %reduce-scatter.14.cloned.1.call-update) | async-done | bytes 2097168 | tf_op jit(solution)/shard_map/reduce_scatter | solution.py:268
  1892.9 153.9 %all-reduce.14.cloned.1.call-done = (bf16[2048,3,256]{2,0,1:T(8,128)(2,1)}, bf16[256,2048]{1,0:T(8,128)(2,1)}) async-done(((bf16[2048,3,256]{2,0,1:T(8,128)(2,1)}, bf16[256,2048]{1,0:T(8,128)(2,1)}), (bf16[2048,3,256]{2,0,1:T(8,128)(2,1)}, bf16[256,2048]{1,0:T(8,128)(2,1)})) %all-reduce.14.cloned.1.call-update) | async-done | bytes 4194320 | tf_op jit(solution)/shard_map/psum | solution.py:350
  2053.7 67.0 %reduce-scatter.12.cloned.1.call-done = bf16[256,2048]{1,0:T(8,128)(2,1)} async-done(((bf16[2048,2048]{1,0:T(8,128)(2,1)}), bf16[256,2048]{1,0:T(8,128)(2,1)}) %reduce-scatter.12.cloned.1.call-update) | async-done | bytes 1048592 | tf_op jit(solution)/shard_map/reduce_scatter | solution.py:332
  2129.3 39.8 %all-reduce.7 = (f32[2048]{0:T(1024)}, f32[128]{0:T(128)}, f32[128]{0:T(128)}, f32[2048]{0:T(1024)}) all-reduce(f32[2048]{0:T(1024)S(1)} %get-tuple-element.250, f32[128]{0:T(128)S(1)} %get-tuple-element.259, f32[128]{0:T(128)S(1)} %get-tuple-element.252, ...), channel_id=1, replica_groups=mesh['expert'=4,'tensor'=8] {'expert','tensor'}, use_global_device_ids=true, to_apply=%region_34.35 | all-reduce | flops 4352 | bytes 34816 | tf_op jit(solution)/shard_map/psum | solution.py:353
  2169.0 82.2 %all-reduce.12.cloned.1.call-done = f32[2048,16]{0,1:T(8,128)} async-done(((f32[2048,16]{0,1:T(8,128)}), f32[2048,16]{0,1:T(8,128)}) %all-reduce.12.cloned.1.call-update) | async-done | bytes 131088 | tf_op jit(solution)/shard_map/psum | solution.py:353
  (376 shorter events, 419.2 us)
Async XLA Ops:
  7.2 87.8 %copy-start = (bf16[256,2048]{1,0:T(8,128)(2,1)S(1)}, bf16[256,2048]{1,0:T(8,128)(2,1)}, u32[]{:S(2)}) copy-start(bf16[256,2048]{1,0:T(8,128)(2,1)} %param.26) | copy-start | bytes 3145732
  7.2 215.0 %reduce-scatter.10.cloned.1.call-start = ((), (), s32[]{:S(2)}) async-start(), calls=%async_computation.9 | async-start | bytes 18874368 | tf_op jit(solution)/shard_map/reduce_scatter | solution.py:184
  103.1 428.6 %all-gather.5.cloned.1.call-start = ((), (), s32[]{:S(2)}) async-start(), calls=%async_computation.10 | async-start | bytes 18874368 | tf_op jit(solution)/shard_map/all_gather | solution.py:231
  103.9 450.5 %all-gather.7.cloned.1.call-start = ((), (), s32[]{:S(2)}) async-start(), calls=%async_computation.11 | async-start | bytes 18874368 | tf_op jit(solution)/shard_map/all_gather | solution.py:232
  104.6 20.8 copy-start.68
  104.7 20.8 copy-start.67
  118.8 107.3 %copy-start.40 = (f32[2048]{0:T(1024)S(1)}, f32[2048]{0:T(1024)}, u32[]{:S(2)}) copy-start(f32[2048]{0:T(1024)} %param.27) | copy-start | bytes 24580
  224.7 20.7 copy-start.52
  226.3 19.1 copy-start.15
  245.4 279.5 %all-to-all-start = ((bf16[4,4,192,2048]{3,2,1,0:T(8,128)(2,1)}), bf16[4,4,192,2048]{3,2,1,0:T(8,128)(2,1)}, u32[]{:S(2)}, u32[]{:S(2)}) async-start(bf16[4,4,192,2048]{3,2,1,0:T(8,128)(2,1)} %bitcast.307), calls=%async_computation.1 | async-start | bytes 25165824 | tf_op jit(solution)/shard_map/all_to_all | solution.py:225
  251.8 325.1 %all-gather.9.cloned.1.call-start = ((), (), s32[]{:S(2)}) async-start(), calls=%async_computation.12 | async-start | bytes 18874368 | tf_op jit(solution)/shard_map/all_gather | solution.py:233
  253.9 23.1 %copy-start.13 = (f32[256,2048]{1,0:T(8,128)}, f32[256,2048]{1,0:T(8,128)S(1)}, u32[]{:S(2)}) copy-start(f32[256,2048]{1,0:T(8,128)S(1)} %convert_element_type.161) | copy-start | bytes 6291460
  257.1 19.9 copy-start.25
  524.9 279.3 %all-to-all-start.2 = ((bf16[4,4,192,2048]{3,2,1,0:T(8,128)(2,1)}), bf16[4,4,192,2048]{3,2,1,0:T(8,128)(2,1)}, u32[]{:S(2)}, u32[]{:S(2)}) async-start(bf16[4,4,192,2048]{3,2,1,0:T(8,128)(2,1)} %bitcast.308), calls=%async_computation.3 | async-start | bytes 25165824 | tf_op jit(solution)/shard_map/all_to_all | solution.py:226
  869.2 278.8 %all-to-all-start.1 = ((bf16[4,4,192,2048]{3,2,1,0:T(8,128)(2,1)}), bf16[4,4,192,2048]{3,2,1,0:T(8,128)(2,1)}, u32[]{:S(2)}, u32[]{:S(2)}) async-start(bf16[4,4,192,2048]{3,2,1,0:T(8,128)(2,1)} %copy.127), calls=%async_computation.2 | async-start | bytes 25165824 | tf_op jit(solution)/shard_map/all_to_all | solution.py:273
  932.3 222.1 %copy-start.51 = (s32[2048,1]{0,1:T(1,128)S(1)}, s32[2048,1]{0,1:T(1,128)}, u32[]{:S(2)}) copy-start(s32[2048,1]{0,1:T(1,128)} %get-tuple-element.337) | copy-start | bytes 24580
  1148.0 278.8 %all-to-all-start.3 = ((bf16[4,4,192,2048]{3,2,1,0:T(8,128)(2,1)}), bf16[4,4,192,2048]{3,2,1,0:T(8,128)(2,1)}, u32[]{:S(2)}, u32[]{:S(2)}) async-start(bf16[4,4,192,2048]{3,2,1,0:T(8,128)(2,1)} %copy.130), calls=%async_computation.4 | async-start | bytes 25165824 | tf_op jit(solution)/shard_map/all_to_all | solution.py:274
  1154.3 470.8 %all-gather.11.cloned.1.call-start = ((), (), s32[]{:S(2)}) async-start(), calls=%async_computation.13 | async-start | bytes 9437184 | tf_op jit(solution)/shard_map/all_gather | solution.py:307
  1154.4 22.9 %copy-start.14 = (f32[256,2048]{1,0:T(8,128)S(1)}, f32[256,2048]{1,0:T(8,128)}, u32[]{:S(2)}) copy-start(f32[256,2048]{1,0:T(8,128)} %copy-done.13) | copy-start | bytes 6291460
  1154.4 22.9 %copy-start.26 = (f32[256,8]{1,0:T(8,128)S(1)}, f32[256,8]{1,0:T(8,128)}, u32[]{:S(2)}) copy-start(f32[256,8]{1,0:T(8,128)} %copy-done.25) | copy-start | bytes 24580
  1187.0 274.3 %copy-start.44 = (bf16[256,16]{0,1:T(8,128)(2,1)}, bf16[256,16]{0,1:T(8,128)(2,1)S(1)}, u32[]{:S(2)}) copy-start(bf16[256,16]{0,1:T(8,128)(2,1)S(1)} %multiply_convert_fusion.5) | copy-start | bytes 24580
  1464.3 22.8 %copy-start.61 = (f32[256]{0:T(256)}, f32[256]{0:T(256)S(1)}, u32[]{:S(2)}) copy-start(f32[256]{0:T(256)S(1)} %broadcast_multiply_fusion.1) | copy-start | bytes 3076
  1467.4 371.4 %reduce-scatter.16.cloned.1.call-start = ((), (), s32[]{:S(2)}) async-start(), calls=%async_computation.17 | async-start | bytes 18874368
  1534.7 314.4 %reduce-scatter.18.cloned.1.call-start = ((), (), s32[]{:S(2)}) async-start(), calls=%async_computation.18 | async-start | bytes 18874368
  1603.4 285.4 %reduce-scatter.14.cloned.1.call-start = ((), (), s32[]{:S(2)}) async-start(), calls=%async_computation.16 | async-start | bytes 18874368 | tf_op jit(solution)/shard_map/reduce_scatter | solution.py:268
  1625.0 421.8 %all-reduce.14.cloned.1.call-start = ((), (), s32[]{:S(2)}) async-start(), calls=%async_computation.19 | async-start | bytes 8388608 | tf_op jit(solution)/shard_map/psum | solution.py:350
  1824.8 295.9 %reduce-scatter.12.cloned.1.call-start = ((), (), s32[]{:S(2)}) async-start(), calls=%async_computation.14 | async-start | bytes 9437184 | tf_op jit(solution)/shard_map/reduce_scatter | solution.py:332
  1836.6 414.6 %all-reduce.12.cloned.1.call-start = ((), (), s32[]{:S(2)}) async-start(), calls=%async_computation.15 | async-start | bytes 262144 | tf_op jit(solution)/shard_map/psum | solution.py:353
  2046.8 76.4 %copy-start.8 = (f32[256,2048]{1,0:T(8,128)S(1)}, f32[256,2048]{1,0:T(8,128)}, u32[]{:S(2)}) copy-start(f32[256,2048]{1,0:T(8,128)} %copy-done.6) | copy-start | bytes 6291460
  2046.8 76.4 %copy-start.42 = (f32[2048]{0:T(1024)S(1)}, f32[2048]{0:T(1024)}, u32[]{:S(2)}) copy-start(f32[2048]{0:T(1024)} %param.27) | copy-start | bytes 24580
  2046.8 76.4 %copy-start.54 = (f32[256]{0:T(256)S(1)}, f32[256]{0:T(256)}, u32[]{:S(2)}) copy-start(f32[256]{0:T(256)} %copy-done.52) | copy-start | bytes 3076
  2046.8 76.4 %copy-start.62 = (f32[256]{0:T(256)S(1)}, f32[256]{0:T(256)}, u32[]{:S(2)}) copy-start(f32[256]{0:T(256)} %copy-done.61) | copy-start | bytes 3076
  (71 other events, 442.6 us)
Sparse Core Ops, SparseCore 0:
  103.2 118.8 reduce-scatter.9
  224.0 93.0 all-gather.4
  319.0 93.0 all-gather.6
  413.8 89.7 all-gather.8
  1467.5 52.3 all-gather.10
  1534.8 114.4 reduce-scatter.15
  1652.8 116.1 reduce-scatter.17
  1772.6 116.1 reduce-scatter.13
  1891.8 154.9 all-reduce.13
  2050.1 70.4 reduce-scatter.11
  2126.8 124.4 all-reduce.11
where the time goes:
time: 2270 us; the launch traced here: 2260 us
  waiting for transfers between devices  1360 us (60%)
  matrix products  361 us (16%)
  local copies, waits for them, and re-layouts  310 us (14%)
  other arithmetic  145 us (6%)
  blocking collectives  39.8 us (2%)
  starting transfers between devices  26.5 us (1%)
    all_to_all x1, waiting for transfers between devices, body(): lax.all_to_all(send_in.reshape(layout), 'expert', split_axis=0, concat_ax...  248 us
    all_to_all x1, waiting for transfers between devices, body(): lax.all_to_all(grad_inputs, 'expert', split_axis=0, concat_axis=0, tiled=...  240 us
    all_to_all x1, waiting for transfers between devices, body(): lax.all_to_all(send_grad.reshape(layout), 'expert', split_axis=0, concat_...  227 us
    all_to_all x1, waiting for transfers between devices, body(): lax.all_to_all(expert_out, 'expert', split_axis=0, concat_axis=0, tiled=T...  216 us
    psum x1, waiting for transfers between devices, body(): lax.psum(qkv_part.astype(jnp.bfloat16), 'expert').astype(jnp.float32)  154 us
    unnamed x156, local copies, waits for them, and re-layouts  146 us
    reduce_scatter x1, waiting for transfers between devices, body(): lax.psum_scatter(jnp.dot(row_part, w_out, preferred_element_type=jnp.floa...  96.5 us
    psum x1, waiting for transfers between devices, body(): lax.psum((attn_gain_part, q_gain_part, k_gain_part, ffn_gain_part, router...  82.2 us
  transfers between devices with their start and end apart: 15, of which 9 were waited for; matrix products, arithmetic and copies ran while one was open for 26% of the time, Pallas kernels for 0%

commit v1 on v0

--- a/solution.py
+++ b/solution.py
@@ -347,7 +347,9 @@
         * jnp.mean(scaled_one * input_own, axis=-1, keepdims=True)
     )
     grad_qkv_sum, grad_out_sum = (
-        lax.psum(qkv_part.astype(jnp.bfloat16), "expert").astype(jnp.float32),
+        jnp.sum(lax.all_gather(qkv_part.astype(jnp.bfloat16), "expert"), axis=0).astype(
+            jnp.float32
+        ),
         lax.psum(out_part.astype(jnp.bfloat16), "expert").astype(jnp.float32),
     )
     grad_attn_gain, grad_q_gain, grad_k_gain, grad_ffn_gain, grad_router = lax.psum(

time: 2270 us -> 2390 us (1.053)
  waiting for transfers between devices: 1360 us -> 1450 us
    all_gather x0 -> x1, waiting for transfers between devices: none -> 159 us  [body(): lax.all_gather(qkv_part.astype(jnp.bfloat16), 'expert')]
    psum x1, waiting for transfers between devices: 154 us -> 50.8 us  [body(): lax.psum(out_part.astype(jnp.bfloat16), 'expert').astype(jnp.float32)]
    psum x1, waiting for transfers between devices: 82.2 us -> 115 us  [body(): lax.psum((attn_gain_part, q_gain_part, k_gain_part, ffn_gain_part, router...]
    unnamed x156 -> x150, local copies, waits for them, and re-layouts: 146 us -> 146 us
  transfers between devices with their start and end apart: 15 -> 16, of which waited for: 9 -> 10; matrix products, arithmetic and copies ran while one was open for 26% -> 26% of each run, Pallas kernels for 0% -> 0%
where the time goes in v1:
time: 2390 us; the launch traced here: 2380 us
  waiting for transfers between devices  1450 us (61%)
  matrix products  366 us (15%)
  local copies, waits for them, and re-layouts  310 us (13%)
  other arithmetic  154 us (6%)
  blocking collectives  53.8 us (2%)
  starting transfers between devices  26.8 us (1%)
    all_to_all x1, waiting for transfers between devices, body(): lax.all_to_all(send_in.reshape(layout), 'expert', split_axis=0, concat_ax...  248 us
    all_to_all x1, waiting for transfers between devices, body(): lax.all_to_all(grad_inputs, 'expert', split_axis=0, concat_axis=0, tiled=...  240 us
    all_to_all x1, waiting for transfers between devices, body(): lax.all_to_all(send_grad.reshape(layout), 'expert', split_axis=0, concat_...  227 us
    all_to_all x1, waiting for transfers between devices, body(): lax.all_to_all(expert_out, 'expert', split_axis=0, concat_axis=0, tiled=T...  216 us
    all_gather x1, waiting for transfers between devices, body(): lax.all_gather(qkv_part.astype(jnp.bfloat16), 'expert')  159 us
    unnamed x150, local copies, waits for them, and re-layouts  146 us
    psum x1, waiting for transfers between devices, body(): lax.psum((attn_gain_part, q_gain_part, k_gain_part, ffn_gain_part, router...  115 us
    reduce_scatter x1, waiting for transfers between devices, body(): lax.psum_scatter(jnp.dot(row_part, w_out, preferred_element_type=jnp.floa...  96.5 us
  transfers between devices with their start and end apart: 16, of which 10 were waited for; matrix products, arithmetic and copies ran while one was open for 26% of the time, Pallas kernels for 0%

profile of v1, /device:TPU:0, one launch (start us, length us, event | category | flops | bytes accessed | tf_op | source)
XLA Modules:
  0.0 2375.7 jit_solution(16182679362215101487)
XLA Ops:
  49.7 41.0 %while.27 = (s32[]{:T(128)}, bf16[4,512,2,128]{3,1,2,0:T(8,128)(2,1)}, f32[4,2,512]{2,1,0:T(2,128)}, s32[4,512]{1,0:T(4,128)S(1)}, s32[2048]{0:T(1024)S(1)}, /*i...) while((s32[]{:T(128)}, ...), condition=%wide.region_9.10_spmd, body=%wide.region_6.9_spmd.sunk | while | flops 1099955200 | bytes 32292448 | solution.py:79
  104.4 14.1 convert_element_type.148
  125.4 96.5 %reduce-scatter.10.cloned.1.call-done = f32[256,2048]{1,0:T(8,128)} async-done(((f32[2048,2048]{1,0:T(8,128)}), f32[256,2048]{1,0:T(8,128)}) %reduce-scatter.10.cloned.1.call-update) | async-done | bytes 2097168 | tf_op jit(solution)/shard_map/reduce_scatter | solution.py:184
  226.0 19.1 scatter_custom_fusion
  256.9 19.8 scatter_custom_fusion.1
  276.7 247.9 %all-to-all-done = bf16[4,4,192,2048]{3,2,1,0:T(8,128)(2,1)} async-done(((bf16[4,4,192,2048]{3,2,1,0:T(8,128)(2,1)}), bf16[4,4,192,2048]{3,2,1,0:T(8,128)(2,1)}, u32[]{:S(2)}, u32[]{:S(2)}) %all-to-all-start) | async-done | bytes 12582944 | tf_op jit(solution)/shard_map/all_to_all | solution.py:225
  531.2 22.6 fusion.42
  553.7 22.5 fusion.38
  576.3 227.4 %all-to-all-done.2 = bf16[4,4,192,2048]{3,2,1,0:T(8,128)(2,1)} async-done(((bf16[4,4,192,2048]{3,2,1,0:T(8,128)(2,1)}), bf16[4,4,192,2048]{3,2,1,0:T(8,128)(2,1)}, u32[]{:S(2)}, u32[]{:S(2)}) %all-to-all-start.2) | async-done | bytes 12582944 | tf_op jit(solution)/shard_map/all_to_all | solution.py:226
  803.6 31.3 %fusion.52 = (bf16[4,4,192,1024]{3,2,0,1:T(8,128)(2,1)}, bf16[4,4,192,1024]{3,2,0,1:T(8,128)(2,1)}, bf16[4,4,192,1024]{3,2,0,1:T(8,128)(2,1)}) fusion(f32[4,4,192,1024]{3,2,1,0:T(8,128)} %fusion.38, f32[4,4,192,1024]{3,2,1,0:T(8,128)} %fusion.42, bf16[4,1024,2048]{2,1,0:T(8,128)(2,1)} %all-gather.11.cloned.1.call-done, ...), kind=kOutput, calls=%fused_computation.79 | convolution fusion | flops 12935233536 | bytes 73400320 | tf_op jit(solution)/shard_map/sctd,cfd->sctf/dot_general | solution.py:243
  834.9 23.0 convert_bitcast_fusion
  874.9 21.8 fusion.36
  896.7 24.3 %fusion.49 = bf16[4,4,192,2048]{3,2,0,1:T(8,128)(2,1)} fusion(f32[4,4,192,2048]{3,2,1,0:T(8,128)} %fusion.36, bf16[4,4,192,1024]{3,2,0,1:T(8,128)(2,1)} %get-tuple-element.312, bf16[4,2048,1024]{2,1,0:T(8,128)(2,1)} %all-gather.7.cloned.1.call-done), kind=kOutput, calls=%fused_computation.74 | convolution fusion | flops 12897484800 | bytes 60817408 | tf_op jit(solution)/shard_map/sctf,cdf->sctd/dot_general | solution.py:256
  931.7 215.7 %all-to-all-done.1 = bf16[4,4,192,2048]{3,2,1,0:T(8,128)(2,1)} async-done(((bf16[4,4,192,2048]{3,2,1,0:T(8,128)(2,1)}), bf16[4,4,192,2048]{3,2,1,0:T(8,128)(2,1)}, u32[]{:S(2)}, u32[]{:S(2)}) %all-to-all-start.1) | async-done | bytes 12582944 | tf_op jit(solution)/shard_map/all_to_all | solution.py:273
  1153.8 23.1 gather_fusion
  1186.6 239.7 %all-to-all-done.3 = bf16[4,4,192,2048]{3,2,1,0:T(8,128)(2,1)} async-done(((bf16[4,4,192,2048]{3,2,1,0:T(8,128)(2,1)}), bf16[4,4,192,2048]{3,2,1,0:T(8,128)(2,1)}, u32[]{:S(2)}, u32[]{:S(2)}) %all-to-all-start.3) | async-done | bytes 12582944 | tf_op jit(solution)/shard_map/all_to_all | solution.py:274
  1426.3 22.7 gather_fusion.1
  1466.6 19.8 bitcast_convert_fusion.2
  1486.4 28.9 %copy.149 = bf16[4,2048,1024]{1,0,2:T(4,128)(2,1)} copy(bf16[4,2048,1024]{2,1,0:T(8,128)(2,1)} %bitcast_convert_fusion.2) | data formatting | bytes 33554432
  1515.3 18.6 copy.184
  1533.9 20.4 bitcast_convert_fusion.1
  1554.3 29.2 %copy.151 = bf16[4,2048,1024]{1,0,2:T(4,128)(2,1)} copy(bf16[4,2048,1024]{2,1,0:T(8,128)(2,1)} %bitcast_convert_fusion.1) | data formatting | bytes 33554432
  1583.5 18.9 copy.185
  1602.5 21.8 bitcast_convert_fusion
  1631.4 165.0 %while.28 = (s32[]{:T(128)}, f32[2048,2,128]{0,2,1:T(8,128)}, f32[2048,2,128]{0,2,1:T(8,128)}, f32[4,512,2,128]{1,0,3,2:T(4,128)}, bf16[4,512,2,128]{3,1,2,0:T(8...) while((s32[]{:T(128)}, f32[2048,2,128]{0,2,1:T(8,128)}, ...), condition=%wide.region_28.29_spmd.clone, body=%wide.region_26.28_spmd.clone.sunk | while | flops 2719611904 | bytes 170962192 | solution.py:125
  1828.7 12.2 fusion.83
  1862.8 25.3 %reduce-scatter.14.cloned.1.call-done = bf16[4,128,2048]{2,1,0:T(8,128)(2,1)} async-done(((bf16[4,1024,2048]{2,1,0:T(8,128)(2,1)}), bf16[4,128,2048]{2,1,0:T(8,128)(2,1)}) %reduce-scatter.14.cloned.1.call-update) | async-done | bytes 2097168 | tf_op jit(solution)/shard_map/reduce_scatter | solution.py:268
  1892.2 50.8 %all-reduce.11.cloned.1.call-done = bf16[256,2048]{1,0:T(8,128)(2,1)} async-done(((bf16[256,2048]{1,0:T(8,128)(2,1)}), bf16[256,2048]{1,0:T(8,128)(2,1)}) %all-reduce.11.cloned.1.call-update) | async-done | bytes 1048592 | tf_op jit(solution)/shard_map/psum | solution.py:353
  1945.8 71.3 %reduce-scatter.12.cloned.1.call-done = bf16[256,2048]{1,0:T(8,128)(2,1)} async-done(((bf16[2048,2048]{1,0:T(8,128)(2,1)}), bf16[256,2048]{1,0:T(8,128)(2,1)}) %reduce-scatter.12.cloned.1.call-update) | async-done | bytes 1048592 | tf_op jit(solution)/shard_map/reduce_scatter | solution.py:332
  2025.8 53.8 %all-reduce.7 = (f32[2048]{0:T(1024)}, f32[128]{0:T(128)}, f32[128]{0:T(128)}, f32[2048]{0:T(1024)}) all-reduce(f32[2048]{0:T(1024)S(1)} %get-tuple-element.250, f32[128]{0:T(128)S(1)} %get-tuple-element.259, f32[128]{0:T(128)S(1)} %get-tuple-element.252, ...), channel_id=1, replica_groups=mesh['expert'=4,'tensor'=8] {'expert','tensor'}, use_global_device_ids=true, to_apply=%region_34.35 | all-reduce | flops 4352 | bytes 34816 | tf_op jit(solution)/shard_map/psum | solution.py:355
  2079.5 158.9 %all-gather.15.cloned.1.call-done = bf16[8192,3,256]{2,0,1:T(8,128)(2,1)} async-done(((bf16[2048,3,256]{2,0,1:T(8,128)(2,1)}), bf16[8192,3,256]{2,0,1:T(8,128)(2,1)}) %all-gather.15.cloned.1.call-update) | async-done | bytes 12582928 | tf_op jit(solution)/shard_map/all_gather | solution.py:350
  2252.6 114.5 %all-reduce.13.cloned.1.call-done = f32[2048,16]{0,1:T(8,128)} async-done(((f32[2048,16]{0,1:T(8,128)}), f32[2048,16]{0,1:T(8,128)}) %all-reduce.13.cloned.1.call-update) | async-done | bytes 131088 | tf_op jit(solution)/shard_map/psum | solution.py:355
  (372 shorter events, 444.1 us)
Async XLA Ops:
  7.2 87.6 %copy-start = (bf16[256,2048]{1,0:T(8,128)(2,1)S(1)}, bf16[256,2048]{1,0:T(8,128)(2,1)}, u32[]{:S(2)}) copy-start(bf16[256,2048]{1,0:T(8,128)(2,1)} %param.26) | copy-start | bytes 3145732
  7.2 214.7 %reduce-scatter.10.cloned.1.call-start = ((), (), s32[]{:S(2)}) async-start(), calls=%async_computation.9 | async-start | bytes 18874368 | tf_op jit(solution)/shard_map/reduce_scatter | solution.py:184
  102.9 428.3 %all-gather.7.cloned.1.call-start = ((), (), s32[]{:S(2)}) async-start(), calls=%async_computation.10 | async-start | bytes 18874368 | tf_op jit(solution)/shard_map/all_gather | solution.py:231
  103.6 450.1 %all-gather.9.cloned.1.call-start = ((), (), s32[]{:S(2)}) async-start(), calls=%async_computation.11 | async-start | bytes 18874368 | tf_op jit(solution)/shard_map/all_gather | solution.py:232
  104.4 20.8 copy-start.69
  104.4 20.9 copy-start.68
  118.5 107.3 %copy-start.41 = (f32[2048]{0:T(1024)S(1)}, f32[2048]{0:T(1024)}, u32[]{:S(2)}) copy-start(f32[2048]{0:T(1024)} %param.27) | copy-start | bytes 24580
  224.5 20.6 copy-start.53
  245.1 279.5 %all-to-all-start = ((bf16[4,4,192,2048]{3,2,1,0:T(8,128)(2,1)}), bf16[4,4,192,2048]{3,2,1,0:T(8,128)(2,1)}, u32[]{:S(2)}, u32[]{:S(2)}) async-start(bf16[4,4,192,2048]{3,2,1,0:T(8,128)(2,1)} %bitcast.308), calls=%async_computation.1 | async-start | bytes 25165824 | tf_op jit(solution)/shard_map/all_to_all | solution.py:225
  251.5 324.7 %all-gather.11.cloned.1.call-start = ((), (), s32[]{:S(2)}) async-start(), calls=%async_computation.12 | async-start | bytes 18874368 | tf_op jit(solution)/shard_map/all_gather | solution.py:233
  253.6 23.1 copy-start.14
  256.8 19.9 copy-start.27
  524.6 279.0 %all-to-all-start.2 = ((bf16[4,4,192,2048]{3,2,1,0:T(8,128)(2,1)}), bf16[4,4,192,2048]{3,2,1,0:T(8,128)(2,1)}, u32[]{:S(2)}, u32[]{:S(2)}) async-start(bf16[4,4,192,2048]{3,2,1,0:T(8,128)(2,1)} %bitcast.309), calls=%async_computation.3 | async-start | bytes 25165824 | tf_op jit(solution)/shard_map/all_to_all | solution.py:226
  868.6 278.8 %all-to-all-start.1 = ((bf16[4,4,192,2048]{3,2,1,0:T(8,128)(2,1)}), bf16[4,4,192,2048]{3,2,1,0:T(8,128)(2,1)}, u32[]{:S(2)}, u32[]{:S(2)}) async-start(bf16[4,4,192,2048]{3,2,1,0:T(8,128)(2,1)} %copy.127), calls=%async_computation.2 | async-start | bytes 25165824 | tf_op jit(solution)/shard_map/all_to_all | solution.py:273
  931.7 222.1 %copy-start.52 = (s32[2048,1]{0,1:T(1,128)S(1)}, s32[2048,1]{0,1:T(1,128)}, u32[]{:S(2)}) copy-start(s32[2048,1]{0,1:T(1,128)} %get-tuple-element.335) | copy-start | bytes 24580
  1147.4 278.8 %all-to-all-start.3 = ((bf16[4,4,192,2048]{3,2,1,0:T(8,128)(2,1)}), bf16[4,4,192,2048]{3,2,1,0:T(8,128)(2,1)}, u32[]{:S(2)}, u32[]{:S(2)}) async-start(bf16[4,4,192,2048]{3,2,1,0:T(8,128)(2,1)} %copy.130), calls=%async_computation.4 | async-start | bytes 25165824 | tf_op jit(solution)/shard_map/all_to_all | solution.py:274
  1153.7 470.7 %all-gather.13.cloned.1.call-start = ((), (), s32[]{:S(2)}) async-start(), calls=%async_computation.13 | async-start | bytes 9437184 | tf_op jit(solution)/shard_map/all_gather | solution.py:307
  1153.8 23.1 copy-start.15
  1153.8 23.1 copy-start.28
  1186.6 273.8 %copy-start.45 = (bf16[256,16]{0,1:T(8,128)(2,1)}, bf16[256,16]{0,1:T(8,128)(2,1)S(1)}, u32[]{:S(2)}) copy-start(bf16[256,16]{0,1:T(8,128)(2,1)S(1)} %multiply_convert_fusion.5) | copy-start | bytes 24580
  1463.5 22.8 copy-start.62
  1466.6 375.7 %reduce-scatter.16.cloned.1.call-start = ((), (), s32[]{:S(2)}) async-start(), calls=%async_computation.19 | async-start | bytes 18874368
  1533.9 318.6 %reduce-scatter.18.cloned.1.call-start = ((), (), s32[]{:S(2)}) async-start(), calls=%async_computation.20 | async-start | bytes 18874368
  1602.5 285.7 %reduce-scatter.14.cloned.1.call-start = ((), (), s32[]{:S(2)}) async-start(), calls=%async_computation.17 | async-start | bytes 18874368 | tf_op jit(solution)/shard_map/reduce_scatter | solution.py:268
  1624.3 318.7 %all-reduce.11.cloned.1.call-start = ((), (), s32[]{:S(2)}) async-start(), calls=%async_computation.15 | async-start | bytes 2097152 | tf_op jit(solution)/shard_map/psum | solution.py:353
  1807.5 209.6 %reduce-scatter.12.cloned.1.call-start = ((), (), s32[]{:S(2)}) async-start(), calls=%async_computation.14 | async-start | bytes 9437184 | tf_op jit(solution)/shard_map/reduce_scatter | solution.py:332
  1828.0 410.5 %all-gather.15.cloned.1.call-start = ((), (), s32[]{:S(2)}) async-start(), calls=%async_computation.18 | async-start | bytes 15728640 | tf_op jit(solution)/shard_map/all_gather | solution.py:350
  1840.9 526.1 %all-reduce.13.cloned.1.call-start = ((), (), s32[]{:S(2)}) async-start(), calls=%async_computation.16 | async-start | bytes 262144 | tf_op jit(solution)/shard_map/psum | solution.py:355
  1862.8 156.9 %copy-start.9 = (f32[256,2048]{1,0:T(8,128)S(1)}, f32[256,2048]{1,0:T(8,128)}, u32[]{:S(2)}) copy-start(f32[256,2048]{1,0:T(8,128)} %copy-done.7) | copy-start | bytes 6291460
  1862.8 156.9 %copy-start.43 = (f32[2048]{0:T(1024)S(1)}, f32[2048]{0:T(1024)}, u32[]{:S(2)}) copy-start(f32[2048]{0:T(1024)} %param.27) | copy-start | bytes 24580
  1862.8 156.9 %copy-start.55 = (f32[256]{0:T(256)S(1)}, f32[256]{0:T(256)}, u32[]{:S(2)}) copy-start(f32[256]{0:T(256)} %copy-done.53) | copy-start | bytes 3076
  1862.8 156.9 %copy-start.63 = (f32[256]{0:T(256)S(1)}, f32[256]{0:T(256)}, u32[]{:S(2)}) copy-start(f32[256]{0:T(256)} %copy-done.62) | copy-start | bytes 3076
  (69 other events, 446.2 us)
Sparse Core Ops, SparseCore 0:
  103.0 118.8 reduce-scatter.9
  223.8 93.0 all-gather.6
  318.7 93.0 all-gather.8
  413.5 89.7 all-gather.10
  1466.7 52.3 all-gather.12
  1534.0 114.4 reduce-scatter.15
  1652.1 116.1 reduce-scatter.17
  1771.9 116.1 reduce-scatter.13
  1891.1 51.8 all-reduce.10
  1946.3 70.7 reduce-scatter.11
  2019.3 219.1 all-gather.14
  2244.4 122.5 all-reduce.12
